TPU v7x, 256 devices: a whole 4x4x8 slice. The times are simulated.
256 devices in a mesh: zero: 32 (over y, x, core), tp: 8 (over z).
Axes of the slice: x: 4, y: 4, z: 8, core: 2. Of those that a mesh axis runs over, the one named last changes fastest.
Arguments:
- weight_gate: bfloat16 [2560, 9728], P('zero', 'tp'), may hold values from -0.125 to 0.125
- low_gate: bfloat16 [2560, 16], P('zero'), may hold values from -0.125 to 0.125
- high_gate: bfloat16 [16, 9728], P(None, 'tp'), may hold values from -1.5 to 1.5
- weight_up: bfloat16 [2560, 9728], P('zero', 'tp'), may hold values from -0.125 to 0.125
- low_up: bfloat16 [2560, 16], P('zero'), may hold values from -0.125 to 0.125
- high_up: bfloat16 [16, 9728], P(None, 'tp'), may hold values from -1.5 to 1.5
- weight_down: bfloat16 [9728, 2560], P('tp', 'zero'), may hold values from -0.0625 to 0.0625
- low_down: bfloat16 [9728, 16], P('tp'), may hold values from -0.0625 to 0.0625
- high_down: bfloat16 [16, 2560], P(None, 'zero'), may hold values from -1.5 to 1.5
- norm_train: float32 [2560], P(('zero', 'tp')), may hold values from 0.25 to 1.75
- norm_step: float32 [2560], P(('zero', 'tp')), may hold values from -0.3 to 0.3
Outputs:
- ready_gate: bfloat16 [2560, 9728], P(None, 'tp')
- ready_up: bfloat16 [2560, 9728], P(None, 'tp')
- ready_down: bfloat16 [9728, 2560], P('tp')
- serve_norm: bfloat16 [2560], replicated
All inputs are finite; a program needn't handle non-finite values.
Results may differ from a plain program's by a relative error of at most 0.001.
Values may be sent and summed in bfloat16 or wider, within the bound.
A program may use at most 128 MiB of HBM per device.

v0:
```python
import jax
import jax.numpy as jnp
from jax import lax
from jax.sharding import Mesh
from jax.sharding import PartitionSpec as P

ZERO = ("zero_0", "zero_1", "zero_2")
ZERO_TP = ("zero_0", "zero_1", "zero_2", "tp")


mix_rate = 0.5


def turned_gather(arrays, axis, dims):
    turned = [jnp.moveaxis(a, dim, 0) for a, dim in zip(arrays, dims)]
    widths = [t[0].size for t in turned]
    both = jnp.concatenate([t.reshape(-1, w) for t, w in zip(turned, widths)], axis=1)
    out = lax.all_gather(both, axis, axis=0, tiled=True)
    pieces = jnp.split(out, [sum(widths[:k]) for k in range(1, len(widths))], axis=1)
    return tuple(
        (
            jnp.moveaxis(b.reshape(-1, *t.shape[1:]), 0, dim)
            for b, t, dim in zip(pieces, turned, dims)
        )
    )


def laid_out(pieces, dim):
    pieces = jnp.moveaxis(pieces, 0, dim)
    dims = pieces.shape
    return pieces.reshape(*dims[:dim], dims[dim] * dims[dim + 1], *dims[dim + 2 :])


def all_blocks(value, axes, turns):
    pieces = value
    for k in turns:
        pieces = lax.all_gather(pieces, axes[k])
    done = turns[::-1]
    back = [done.index(k) for k in range(len(axes))]
    pieces = pieces.transpose(*back, *range(len(axes), pieces.ndim))
    return pieces.reshape(-1, *value.shape)


def gathered_by_axis(value, axes, turns, dim):
    return laid_out(all_blocks(value, axes, turns), dim)


def local(
    weight_gate,
    low_gate,
    high_gate,
    weight_up,
    low_up,
    high_up,
    weight_down,
    low_down,
    high_down,
    norm_train,
    norm_step,
):
    latest_gate = weight_gate.astype(jnp.float32) + mix_rate * jnp.dot(
        low_gate, high_gate, preferred_element_type=jnp.float32
    )
    latest_up = weight_up.astype(jnp.float32) + mix_rate * jnp.dot(
        low_up, high_up, preferred_element_type=jnp.float32
    )
    latest_down = weight_down.astype(jnp.float32) + mix_rate * jnp.dot(
        low_down, high_down, preferred_element_type=jnp.float32
    )
    narrow_gate, narrow_up, narrow_down = (
        latest_gate.astype(jnp.bfloat16),
        latest_up.astype(jnp.bfloat16),
        latest_down.astype(jnp.bfloat16),
    )
    ready_gate, ready_up, ready_down = turned_gather(
        (narrow_gate, narrow_up, narrow_down), ZERO, (0, 0, 1)
    )
    serve_norm = gathered_by_axis(
        (norm_train + norm_step).astype(jnp.bfloat16), ZERO_TP, (0, 1, 3, 2), 0
    )
    return (ready_gate, ready_up, ready_down, serve_norm)


def solution(mesh):
    finer = Mesh(
        mesh.devices.reshape(4, 4, 2, mesh.shape["tp"]), ("zero_0", "zero_1", "zero_2", "tp")
    )
    return jax.shard_map(
        local,
        mesh=finer,
        in_specs=(
            P(ZERO, "tp"),
            P(ZERO, None),
            P(None, "tp"),
            P(ZERO, "tp"),
            P(ZERO, None),
            P(None, "tp"),
            P("tp", ZERO),
            P("tp", None),
            P(None, ZERO),
            P(ZERO_TP),
            P(ZERO_TP),
        ),
        out_specs=(P(None, "tp"), P(None, "tp"), P("tp", None), P()),
        check_vma=False,
    )
```

profile of v0, /device:TPU:1, one launch (start us, length us, event | category | flops | bytes accessed | tf_op | source)
XLA Modules:
  0.0 150.4 jit_solution(1845330764220144492)
XLA Ops:
  7.2 0.0 copy-start
  7.2 0.0 all-gather.7.cloned.1.call-start
  7.2 0.7 copy-done
  8.0 1.2 fusion.3
  9.1 1.2 fusion.4
  10.4 1.2 fusion.6
  11.6 1.1 concatenate.3
  12.7 0.0 all-gather.7.cloned.1.call-update
  12.7 1.3 dynamic-slice
  14.6 0.7 add_convert_fusion
  15.3 0.2 dynamic-update-slice
  15.5 9.5 %all-reduce = bf16[40]{0:T(256)(128)(2,1)S(1)} all-reduce(bf16[40]{0:T(256)(128)(2,1)S(1)} %dynamic-update-slice), channel_id=2, replica_groups=mesh['zero_0'=4,'zero_1'=4,'zero_2'=2,'tp'=8] {'zero_0'}, use_global_device_ids=true, to_apply=%add | all-reduce | flops 40 | bytes 160
  25.0 0.1 reshape.15
  25.1 7.7 %all-gather.4 = bf16[4,4,10]{2,1,0:T(4,128)(2,1)S(1)} all-gather(bf16[1,4,10]{2,1,0:T(4,128)(2,1)S(1)} %reshape.15), channel_id=3, replica_groups=mesh['zero_0'=4,'zero_1'=4,'zero_2'=2,'tp'=8] {'zero_1'}, dimensions={0}, use_global_device_ids=true | all-gather | bytes 400 | tf_op jit(solution)/shard_map/all_gather | solution.py:37
  32.8 23.2 %all-gather.2 = bf16[32,4,10]{2,1,0:T(4,128)(2,1)S(1)} all-gather(bf16[4,4,10]{2,1,0:T(4,128)(2,1)S(1)} %all-gather.4), channel_id=4, replica_groups=mesh['zero_0'=4,'zero_1'=4,'zero_2'=2,'tp'=8] {'tp'}, dimensions={0}, use_global_device_ids=true | all-gather | bytes 2880 | tf_op jit(solution)/shard_map/all_gather | solution.py:37
  56.0 11.3 %all-gather.3 = bf16[16,4,4,10]{3,2,1,0:T(4,128)(2,1)S(1)} all-gather(bf16[8,4,4,10]{3,2,1,0:T(4,128)(2,1)S(1)} %bitcast.20), channel_id=5, replica_groups=mesh['zero_0'=4,'zero_1'=4,'zero_2'=2,'tp'=8] {'zero_2'}, dimensions={0}, use_global_device_ids=true | all-gather | bytes 7680 | tf_op jit(solution)/shard_map/all_gather | solution.py:37
  67.3 0.7 reshape_reshape.3
  68.1 31.7 %all-gather.7.cloned.1.call-done = bf16[2560,3648]{1,0:T(8,128)(2,1)} async-done(((bf16[80,3648]{1,0:T(8,128)(2,1)}), bf16[2560,3648]{1,0:T(8,128)(2,1)}) %all-gather.7.cloned.1.call-update) | async-done | bytes 18677776 | tf_op jit(solution)/shard_map/all_gather | solution.py:18
  99.7 15.8 %slice_bitcast_fusion = (bf16[1216,2560]{0,1:T(8,128)(2,1)}, bf16[2560,1216]{1,0:T(8,128)(2,1)}, bf16[2560,1216]{1,0:T(8,128)(2,1)}) fusion(bf16[2560,3648]{1,0:T(8,128)(2,1)} %all-gather.7.cloned.1.call-done), kind=kLoop, calls=%fused_computation | loop fusion | bytes 37355520 | tf_op jit(solution)/shard_map/transpose | solution.py:22
  115.5 9.3 %copy.23 = bf16[2560,1216]{0,1:T(8,128)(2,1)} copy(bf16[2560,1216]{1,0:T(8,128)(2,1)} %get-tuple-element.18) | data formatting | bytes 12451840
  124.9 9.3 %copy.24 = bf16[2560,1216]{0,1:T(8,128)(2,1)} copy(bf16[2560,1216]{1,0:T(8,128)(2,1)} %get-tuple-element.17) | data formatting | bytes 12451840
  134.2 9.3 %copy.25 = bf16[1216,2560]{1,0:T(8,128)(2,1)} copy(bf16[1216,2560]{0,1:T(8,128)(2,1)} %get-tuple-element.16) | data formatting | bytes 12451840
  (2 shorter events, 0.0 us)
Async XLA Ops:
  7.2 0.8 copy-start
  7.2 92.5 %all-gather.7.cloned.1.call-start = ((), (), s32[]{:S(2)}) async-start(), calls=%async_computation | async-start | bytes 19599360 | tf_op jit(solution)/shard_map/all_gather | solution.py:18
Sparse Core Ops, SparseCore 0:
  12.8 86.8 all-gather.6
where the time goes:
time: 151 us; the launch traced here: 150 us
  blocking collectives  51.7 us (34%)
  local copies, waits for them, and re-layouts  47.9 us (32%)
  waiting for transfers between devices  31.7 us (21%)
  between operations  14.7 us (10%)
  matrix products  3.63 us (2%)
    all_gather x3, blocking collectives, all_blocks(): pieces = lax.all_gather(pieces, axes[k])  42.2 us
    all_gather x1, waiting for transfers between devices, turned_gather(): out = lax.all_gather(both, axis, axis=0, tiled=True)  31.7 us
    unnamed x9, local copies, waits for them, and re-layouts  30.3 us
    transpose x1, local copies, waits for them, and re-layouts, turned_gather(): jnp.moveaxis(b.reshape(-1, *t.shape[1:]), 0, dim)  15.8 us
    unnamed x1, blocking collectives  9.52 us
  transfers between devices with their start and end apart: 1, of which 1 were waited for; matrix products, arithmetic and copies ran while one was open for 2% of the time, Pallas kernels for 0%

commit v1 on v0

v1 whole, which is shorter than its diff:
```python
import functools
import heapq

import jax
import jax.numpy as jnp
from jax import lax
from jax.experimental import pallas as pl
from jax.experimental.pallas import tpu as pltpu
from jax.sharding import PartitionSpec as P

MESH = pl.DeviceIdType.MESH
LINKS = ("u+", "u-", "v+", "v-")
SIDE = 4
BLOCK = 80
WIDTH = 1216
RANK = 16
LANE = 128
CHUNKS = {"A0": (0, 7), "A1": (7, 14), "B0": (14, 21), "B1": (21, 29)}
TILES = 29
COLUMNS = TILES * LANE
NORM_LANE = 3 * WIDTH
HALF = LANE // 2

mix_rate = 0.5


def onward(item):
    chunk, ou, ov = item
    first, second = ("u", "v") if chunk[0] == "A" else ("v", "u")
    a, b = (ou, ov) if chunk[0] == "A" else (ov, ou)
    turn = "+" if chunk[1] == "0" else "-"
    far = SIDE - 1 if turn == "+" else 1
    if b == 0:
        out = [first + "+", first + "-"] if a == 0 else [first + turn] if a == far else []
        return out + [second + "+", second + "-"]
    return [second + turn] if b == far else []


def seen_there(item, link):
    chunk, ou, ov = item
    step = SIDE - 1 if link[1] == "+" else 1
    return (chunk, (ou + step) % SIDE, ov) if link[0] == "u" else (chunk, ou, (ov + step) % SIDE)


def depth(item):
    return max((1 + depth(seen_there(item, link)) for link in onward(item)), default=0)


def plan(tile_us=0.44, hop_us=2.5):
    free = dict.fromkeys(LINKS, 0.0)
    ready = {link: [] for link in LINKS}
    sends = {link: [] for link in LINKS}
    arrivals, events, count = [], [], 0
    for chunk in CHUNKS:
        events.append((0.0, count, (chunk, 0, 0)))
        count += 1
    while events:
        now, _, item = heapq.heappop(events)
        if item is not None:
            arrivals.append(item)
            for link in onward(item):
                heapq.heappush(ready[link], (-depth(seen_there(item, link)), count, item))
                count += 1
        if events and events[0][0] <= now + 1e-9:
            continue
        for link in LINKS:
            if free[link] <= now + 1e-9 and ready[link]:
                item = heapq.heappop(ready[link])[2]
                lo, hi = CHUNKS[item[0]]
                free[link] = now + (hi - lo) * tile_us
                sends[link].append(item)
                heapq.heappush(events, (free[link], count, None))
                heapq.heappush(events, (free[link] + hop_us, count + 1, seen_there(item, link)))
                count += 2
    return sends, arrivals


def gather_kernel(
    wg, ag, bg, wu, au, bu, wd, ad, bd, nt, ns, all_ref,
    w, a, b, n, nz, in_sem, recv_sem, norm_send, norm_recv, send_sem, peer_send, peer_recv,
):
    zero, z = lax.axis_index("zero"), lax.axis_index("tp")
    tp = lax.axis_size("tp")
    core, chip = lax.rem(zero, 2), lax.div(zero, 2)
    x, y = lax.rem(chip, SIDE), lax.div(chip, SIDE)

    def at(ou, ov):
        ox = lax.rem(x + (1 - core) * ou - core * ov + SIDE, SIDE)
        oy = lax.rem(y + (1 - core) * ov - core * ou + SIDE, SIDE)
        return (oy * SIDE + ox) * 2 + core

    place = {(ou, ov): at(ou, ov) for ou in range(SIDE) for ov in range(SIDE)}
    target = {"u+": place[1, 0], "u-": place[3, 0], "v+": place[0, 1], "v-": place[0, 3]}
    peer = zero + 1 - 2 * core

    copies = []
    for k, (src, dst) in enumerate(
        [(nt, n.at[0]), (ns, n.at[1])]
        + [
            pair
            for t, refs in enumerate([(wg, ag, bg), (wu, au, bu), (wd, ad, bd)])
            for pair in zip(refs, (w.at[t], a.at[t], b.at[t]))
        ]
    ):
        copy = pltpu.make_async_copy(src, dst, in_sem.at[k])
        copy.start()
        copies.append(copy)

    barrier = pltpu.get_barrier_semaphore()
    others = [lax.rem(z + k, tp) for k in range(1, tp)]
    for other in list(target.values()) + [peer]:
        pl.semaphore_signal(barrier, inc=1, device_id={"zero": other, "tp": z}, device_id_type=MESH)
    for other in others:
        pl.semaphore_signal(barrier, inc=1, device_id={"zero": zero, "tp": other}, device_id_type=MESH)

    copies[0].wait()
    copies[1].wait()
    gain = (n[0] + n[1]).astype(jnp.bfloat16).astype(jnp.float32)
    nz[z] = jnp.concatenate([gain, jnp.zeros((1, LANE - gain.shape[1]), jnp.float32)], axis=1)

    mine = pl.ds(pl.multiple_of(zero * BLOCK, 16), BLOCK)
    latest = []
    for t in range(3):
        for copy in copies[2 + 3 * t : 5 + 3 * t]:
            copy.wait()
        low_high = lax.dot_general(
            a[t], b[t], (((0,), (0,)), ((), ())), preferred_element_type=jnp.float32
        )
        latest.append(w[t].astype(jnp.float32) + mix_rate * low_high)
        if t == 1:
            both = jnp.concatenate(latest, axis=1)
            all_ref[mine, 0 : 2 * WIDTH] = both.astype(jnp.bfloat16)
    cut = WIDTH - HALF
    all_ref[mine, 2 * WIDTH : COLUMNS - LANE] = latest[2][:, :cut].astype(jnp.bfloat16)
    tail = jnp.concatenate([latest[2][:, cut:], jnp.zeros((BLOCK, HALF), jnp.float32)], axis=1)

    pl.semaphore_wait(barrier, len(target) + 1 + len(others))

    norm_copies = []
    for k, other in enumerate(others):
        copy = pltpu.make_async_remote_copy(
            src_ref=nz.at[z], dst_ref=nz.at[z], send_sem=norm_send.at[k], recv_sem=norm_recv.at[k],
            device_id={"zero": zero, "tp": other}, device_id_type=MESH,
        )
        copy.start()
        norm_copies.append(copy)

    def span(item):
        chunk, ou, ov = item
        lo, hi = CHUNKS[chunk]
        rows = pl.ds(pl.multiple_of(place[ou, ov] * BLOCK, 16), BLOCK)
        return all_ref.at[rows, lo * LANE : hi * LANE]

    sends, arrivals = plan()
    number = {item: k for k, item in enumerate(i for i in arrivals if i[1:] != (0, 0))}

    def send(item, link):
        part = span(item)
        pltpu.make_async_remote_copy(
            src_ref=part, dst_ref=part, send_sem=send_sem, recv_sem=recv_sem.at[number[seen_there(item, link)]],
            device_id={"zero": target[link], "tp": z}, device_id_type=MESH,
        ).start()

    def hand_over(item):
        part = span(item)
        pltpu.make_async_remote_copy(
            src_ref=part, dst_ref=part, send_sem=peer_send, recv_sem=peer_recv,
            device_id={"zero": peer, "tp": z}, device_id_type=MESH,
        ).start()

    queue = {link: list(order) for link, order in sends.items()}
    here = set()

    def issue():
        moved = True
        while moved:
            moved = False
            for link in LINKS:
                if queue[link] and queue[link][0] in here:
                    send(queue[link].pop(0), link)
                    moved = True

    here |= {("A0", 0, 0), ("A1", 0, 0), ("B0", 0, 0)}
    issue()

    for copy in norm_copies:
        copy.wait_recv()
    row = lax.broadcasted_iota(jnp.int32, (BLOCK, LANE), 0)
    lane = lax.broadcasted_iota(jnp.int32, (BLOCK, LANE), 1)
    share = BLOCK // tp
    picked = jnp.zeros((BLOCK, LANE), jnp.float32)
    for k in range(tp):
        own = (lane == row - k * share) & (lane < share)
        picked = jnp.where(own, jnp.broadcast_to(nz[k], (BLOCK, LANE)), picked)
    column = jnp.sum(picked, axis=1, keepdims=True)
    tail = jnp.where(lane == HALF, column, tail)
    all_ref[mine, COLUMNS - LANE : COLUMNS] = tail.astype(jnp.bfloat16)
    here.add(("B1", 0, 0))
    issue()
    for chunk in CHUNKS:
        hand_over((chunk, 0, 0))

    for item in arrivals:
        if item[1:] == (0, 0):
            continue
        part = span(item)
        pltpu.make_async_remote_copy(
            src_ref=part, dst_ref=part, send_sem=send_sem, recv_sem=recv_sem.at[number[item]],
            device_id={"zero": peer, "tp": z}, device_id_type=MESH,
        ).wait_recv()
        here.add(item)
        issue()
        hand_over(item)
    assert not any(queue.values())

    blocks = SIDE * SIDE
    for sem, rows in ((peer_recv, blocks), (peer_send, blocks), (send_sem, blocks - 1)):
        whole = all_ref.at[0 : rows * BLOCK]
        pltpu.make_async_copy(whole, whole, sem).wait()
    for copy in norm_copies:
        copy.wait_send()


def turn_kernel(all_ref, gate, up, down, norm, stage, norm_rows, sem, norm_sem):
    outs = (gate, up, down)
    total = all_ref.shape[0]
    size, step = stage.shape[1], LANE
    starts = list(range(0, COLUMNS, size))
    pending = {}
    for order, start in enumerate(starts[-1:] + starts[:-1]):
        wide = min(size, COLUMNS - start)
        slot = order % stage.shape[0]
        for copy in pending.pop(slot, ()):
            copy.wait()

        def body(i, carry):
            rows = pl.ds(pl.multiple_of(i * step, step), step)
            stage[slot, 0:wide, rows] = all_ref[rows, start : start + wide].T
            return carry

        lax.fori_loop(0, total // step, body, 0, unroll=True)
        started = []
        for t in range(3):
            lo, hi = max(start, t * WIDTH), min(start + wide, (t + 1) * WIDTH)
            if lo < hi:
                copy = pltpu.make_async_copy(
                    stage.at[slot, lo - start : hi - start],
                    outs[t].at[lo - t * WIDTH : hi - t * WIDTH],
                    sem.at[slot, len(started)],
                )
                copy.start()
                started.append(copy)
        if start <= NORM_LANE < start + wide:
            row = stage[slot, NORM_LANE - start : NORM_LANE - start + 1, :].astype(jnp.float32)
            pieces = [row[:, k : k + LANE] for k in range(0, total, LANE)]
            norm_rows[...] = jnp.concatenate(pieces, axis=0).astype(jnp.bfloat16)
            copy = pltpu.make_async_copy(norm_rows, norm, norm_sem)
            copy.start()
            started.append(copy)
        pending[slot] = started
    for started in pending.values():
        for copy in started:
            copy.wait()


def local(wg, ag, bg, wu, au, bu, wd, ad, bd, nt, ns):
    rows = 2560
    bf16 = jnp.bfloat16
    hbm = pl.BlockSpec(memory_space=pltpu.HBM)
    inputs = (wg, ag.T, bg, wu, au.T, bu, wd.T, bd, ad.T, nt.reshape(1, -1), ns.reshape(1, -1))
    items = len(CHUNKS) * (SIDE * SIDE - 1)
    gathered = pl.pallas_call(
        gather_kernel,
        out_shape=pltpu.VMEM((rows, COLUMNS), bf16),
        in_specs=[hbm] * 11,
        out_specs=pl.BlockSpec(memory_space=pltpu.VMEM),
        scratch_shapes=[
            pltpu.VMEM((3, BLOCK, WIDTH), bf16),
            pltpu.VMEM((3, RANK, BLOCK), bf16),
            pltpu.VMEM((3, RANK, WIDTH), bf16),
            pltpu.VMEM((2, 1, nt.shape[0]), jnp.float32),
            pltpu.VMEM((8, 1, LANE), jnp.float32),
            pltpu.SemaphoreType.DMA((11,)),
            pltpu.SemaphoreType.DMA((items,)),
            pltpu.SemaphoreType.DMA((7,)),
            pltpu.SemaphoreType.DMA((7,)),
            pltpu.SemaphoreType.DMA,
            pltpu.SemaphoreType.DMA,
            pltpu.SemaphoreType.DMA,
        ],
        compiler_params=pltpu.CompilerParams(collective_id=0, has_side_effects=True, vmem_limit_bytes=16 << 20),
        name="gather",
    )(*(pltpu.with_memory_space_constraint(v, pltpu.HBM) for v in inputs))
    gate, up, down, norm = pl.pallas_call(
        turn_kernel,
        out_shape=[jax.ShapeDtypeStruct((WIDTH, rows), bf16)] * 3 + [jax.ShapeDtypeStruct((rows // LANE, LANE), bf16)],
        in_specs=[pl.BlockSpec(memory_space=pltpu.VMEM)],
        out_specs=[hbm] * 4,
        scratch_shapes=[
            pltpu.VMEM((4, 256, rows), bf16),
            pltpu.VMEM((rows // LANE, LANE), bf16),
            pltpu.SemaphoreType.DMA((4, 2)),
            pltpu.SemaphoreType.DMA,
        ],
        compiler_params=pltpu.CompilerParams(vmem_limit_bytes=16 << 20),
        name="turn",
    )(gathered)
    return gate.T, up.T, down, norm.reshape(rows)


def solution(mesh):
    return jax.shard_map(
        local,
        mesh=mesh,
        in_specs=(
            P("zero", "tp"),
            P("zero", None),
            P(None, "tp"),
            P("zero", "tp"),
            P("zero", None),
            P(None, "tp"),
            P("tp", "zero"),
            P("tp", None),
            P(None, "zero"),
            P(("zero", "tp")),
            P(("zero", "tp")),
        ),
        out_specs=(P(None, "tp"), P(None, "tp"), P("tp", None), P()),
        check_vma=False,
    )
```

time: 151 us -> 70.5 us (0.47)
  Pallas kernels: 0 us -> 69.7 us
  blocking collectives: 51.7 us -> 0 us
  local copies, waits for them, and re-layouts: 47.9 us -> 0 us
  waiting for transfers between devices: 31.7 us -> 0 us
  between operations: 14.7 us -> 0.64 us
  matrix products: 3.63 us -> 0 us
    pallas_call x0 -> x2, Pallas kernels: none -> 69.7 us  [the longest x1 62.8 us: local(): pl.pallas_call(gather_kernel, out_shape=pltpu.VMEM((rows, COLUMNS), bf16)...]
    all_gather x3 -> x0, blocking collectives: 42.2 us -> none  [all_blocks(): pieces = lax.all_gather(pieces, axes[k])]
    all_gather x1 -> x0, waiting for transfers between devices: 31.7 us -> none  [turned_gather(): out = lax.all_gather(both, axis, axis=0, tiled=True)]
    unnamed x9 -> x0, local copies, waits for them, and re-layouts: 30.3 us -> none
    transpose x1 -> x0, local copies, waits for them, and re-layouts: 15.8 us -> none  [turned_gather(): jnp.moveaxis(b.reshape(-1, *t.shape[1:]), 0, dim)]
    unnamed x1 -> x0, blocking collectives: 9.52 us -> none
    dot_general x3 -> x0, matrix products: 3.63 us -> none  [the longest x1 1.23 us: local(): jnp.dot(low_down, high_down, preferred_element_type=jnp.float32)]
  transfers between devices with their start and end apart: 1 -> 0, of which waited for: 1 -> 0; matrix products, arithmetic and copies ran while one was open for 2% -> 0% of each run, Pallas kernels for 0% -> 0%
where the time goes in v1:
time: 70.5 us; the launch traced here: 70.4 us
  Pallas kernels  69.7 us (99%)
    pallas_call x1, Pallas kernels, local(): pl.pallas_call(gather_kernel, out_shape=pltpu.VMEM((rows, COLUMNS), bf16)...  62.8 us
    pallas_call x1, Pallas kernels, local(): pl.pallas_call(turn_kernel, out_shape=[jax.ShapeDtypeStruct((WIDTH, rows)...  6.93 us

profile of v1, /device:TPU:1, one launch (start us, length us, event | category | flops | bytes accessed | tf_op | source)
XLA Modules:
  0.0 70.4 jit_solution(2639507760547584738)
XLA Ops:
  0.6 62.8 %gather.1.all_ref = bf16[2560,3712]{1,0:T(8,128)(2,1)S(1)} custom-call(bf16[80,1216]{1,0:T(8,128)(2,1)} %wg.1, bf16[16,80]{1,0:T(8,128)(2,1)} %bitcast.11, bf16[16,1216]{1,0:T(8,128)(2,1)} %bg.1, bf16[80,1216]{1,0:T(8,128)(2,1)} %wu.1, bf16[16,80]{1,0:T(8,128)(2,1)} %bitcast.12, bf16[16,1216]{1,0:T(8,128)(2,1)} %bu.1, bf16[80,1216]{1,0:T(8,128)(2,1)} %bitcast.9, ...), custom_call_target="tpu_custom_call" | custom-call | tf_op jit(solution)/shard_map/gather/pallas_call | solution.py:272
  63.4 6.9 %turn.1 = (bf16[1216,2560]{1,0:T(8,128)(2,1)}, bf16[1216,2560]{1,0:T(8,128)(2,1)}, bf16[1216,2560]{1,0:T(8,128)(2,1)}, bf16[20,128]{1,0:T(8,128)(2,1)}) custom-call(bf16[2560,3712]{1,0:T(8,128)(2,1)S(1)} %gather.1.all_ref), custom_call_target="tpu_custom_call" | custom-call | tf_op jit(solution)/shard_map/turn/pallas_call | solution.py:294

commit v2 on v1

--- a/solution.py
+++ b/solution.py
@@ -15,7 +15,8 @@
 WIDTH = 1216
 RANK = 16
 LANE = 128
-CHUNKS = {"A0": (0, 7), "A1": (7, 14), "B0": (14, 21), "B1": (21, 29)}
+CHUNKS = {"A0": (0, 7), "B1": (21, 28), "A1": (7, 14), "B0": (14, 21), "C0": (28, 29)}
+OWN_US = {"A0": 0.0, "B1": 0.0, "A1": 0.6, "B0": 0.6, "C0": 20.0}
 TILES = 29
 COLUMNS = TILES * LANE
 NORM_LANE = 3 * WIDTH
@@ -26,8 +27,8 @@
 
 def onward(item):
     chunk, ou, ov = item
-    first, second = ("u", "v") if chunk[0] == "A" else ("v", "u")
-    a, b = (ou, ov) if chunk[0] == "A" else (ov, ou)
+    first, second = ("v", "u") if chunk[0] == "B" else ("u", "v")
+    a, b = (ov, ou) if chunk[0] == "B" else (ou, ov)
     turn = "+" if chunk[1] == "0" else "-"
     far = SIDE - 1 if turn == "+" else 1
     if b == 0:
@@ -52,7 +53,7 @@
     sends = {link: [] for link in LINKS}
     arrivals, events, count = [], [], 0
     for chunk in CHUNKS:
-        events.append((0.0, count, (chunk, 0, 0)))
+        events.append((OWN_US[chunk], count, (chunk, 0, 0)))
         count += 1
     while events:
         now, _, item = heapq.heappop(events)
@@ -77,7 +78,7 @@
 
 def gather_kernel(
     wg, ag, bg, wu, au, bu, wd, ad, bd, nt, ns, all_ref,
-    w, a, b, n, nz, in_sem, recv_sem, norm_send, norm_recv, send_sem, peer_send, peer_recv,
+    w, a, b, n, nz, in_sem, recv_sem, norm_send, norm_recv, ready, send_sem, peer_send, peer_recv,
 ):
     zero, z = lax.axis_index("zero"), lax.axis_index("tp")
     tp = lax.axis_size("tp")
@@ -93,66 +94,52 @@
     target = {"u+": place[1, 0], "u-": place[3, 0], "v+": place[0, 1], "v-": place[0, 3]}
     peer = zero + 1 - 2 * core
 
-    copies = []
+    loads = []
     for k, (src, dst) in enumerate(
-        [(nt, n.at[0]), (ns, n.at[1])]
-        + [
+        [
             pair
-            for t, refs in enumerate([(wg, ag, bg), (wu, au, bu), (wd, ad, bd)])
+            for t, refs in ((0, (wg, ag, bg)), (2, (wd, ad, bd)), (1, (wu, au, bu)))
             for pair in zip(refs, (w.at[t], a.at[t], b.at[t]))
         ]
+        + [(nt, n.at[0]), (ns, n.at[1])]
     ):
-        copy = pltpu.make_async_copy(src, dst, in_sem.at[k])
-        copy.start()
-        copies.append(copy)
+        load = pltpu.make_async_copy(src, dst, in_sem.at[k])
+        load.start()
+        loads.append(load)
 
     barrier = pltpu.get_barrier_semaphore()
-    others = [lax.rem(z + k, tp) for k in range(1, tp)]
     for other in list(target.values()) + [peer]:
         pl.semaphore_signal(barrier, inc=1, device_id={"zero": other, "tp": z}, device_id_type=MESH)
-    for other in others:
-        pl.semaphore_signal(barrier, inc=1, device_id={"zero": zero, "tp": other}, device_id_type=MESH)
-
-    copies[0].wait()
-    copies[1].wait()
-    gain = (n[0] + n[1]).astype(jnp.bfloat16).astype(jnp.float32)
-    nz[z] = jnp.concatenate([gain, jnp.zeros((1, LANE - gain.shape[1]), jnp.float32)], axis=1)
+    for k in range(1, tp):
+
+        @pl.when(k > z)
+        def _():
+            pl.semaphore_signal(barrier, inc=1, device_id={"zero": zero, "tp": k}, device_id_type=MESH)
 
     mine = pl.ds(pl.multiple_of(zero * BLOCK, 16), BLOCK)
-    latest = []
-    for t in range(3):
-        for copy in copies[2 + 3 * t : 5 + 3 * t]:
-            copy.wait()
+    cut = WIDTH - HALF
+
+    def latest(t, order):
+        for load in loads[3 * order : 3 * order + 3]:
+            load.wait()
         low_high = lax.dot_general(
             a[t], b[t], (((0,), (0,)), ((), ())), preferred_element_type=jnp.float32
         )
-        latest.append(w[t].astype(jnp.float32) + mix_rate * low_high)
-        if t == 1:
-            both = jnp.concatenate(latest, axis=1)
-            all_ref[mine, 0 : 2 * WIDTH] = both.astype(jnp.bfloat16)
-    cut = WIDTH - HALF
-    all_ref[mine, 2 * WIDTH : COLUMNS - LANE] = latest[2][:, :cut].astype(jnp.bfloat16)
-    tail = jnp.concatenate([latest[2][:, cut:], jnp.zeros((BLOCK, HALF), jnp.float32)], axis=1)
-
-    pl.semaphore_wait(barrier, len(target) + 1 + len(others))
-
-    norm_copies = []
-    for k, other in enumerate(others):
-        copy = pltpu.make_async_remote_copy(
-            src_ref=nz.at[z], dst_ref=nz.at[z], send_sem=norm_send.at[k], recv_sem=norm_recv.at[k],
-            device_id={"zero": zero, "tp": other}, device_id_type=MESH,
-        )
-        copy.start()
-        norm_copies.append(copy)
+        return w[t].astype(jnp.float32) + mix_rate * low_high
+
+    gate = latest(0, 0)
+    all_ref[mine, 0:cut] = gate[:, :cut].astype(jnp.bfloat16)
+    down = latest(2, 1)
+    all_ref[mine, 2 * WIDTH : 2 * WIDTH + cut] = down[:, :cut].astype(jnp.bfloat16)
+
+    sends, arrivals = plan()
+    number = {item: k for k, item in enumerate(i for i in arrivals if i[1:] != (0, 0))}
 
     def span(item):
         chunk, ou, ov = item
         lo, hi = CHUNKS[chunk]
         rows = pl.ds(pl.multiple_of(place[ou, ov] * BLOCK, 16), BLOCK)
         return all_ref.at[rows, lo * LANE : hi * LANE]
-
-    sends, arrivals = plan()
-    number = {item: k for k, item in enumerate(i for i in arrivals if i[1:] != (0, 0))}
 
     def send(item, link):
         part = span(item)
@@ -171,7 +158,8 @@
     queue = {link: list(order) for link, order in sends.items()}
     here = set()
 
-    def issue():
+    def issue(*items):
+        here.update(items)
         moved = True
         while moved:
             moved = False
@@ -179,46 +167,89 @@
                 if queue[link] and queue[link][0] in here:
                     send(queue[link].pop(0), link)
                     moved = True
-
-    here |= {("A0", 0, 0), ("A1", 0, 0), ("B0", 0, 0)}
-    issue()
-
-    for copy in norm_copies:
-        copy.wait_recv()
-    row = lax.broadcasted_iota(jnp.int32, (BLOCK, LANE), 0)
-    lane = lax.broadcasted_iota(jnp.int32, (BLOCK, LANE), 1)
-    share = BLOCK // tp
-    picked = jnp.zeros((BLOCK, LANE), jnp.float32)
-    for k in range(tp):
-        own = (lane == row - k * share) & (lane < share)
-        picked = jnp.where(own, jnp.broadcast_to(nz[k], (BLOCK, LANE)), picked)
-    column = jnp.sum(picked, axis=1, keepdims=True)
-    tail = jnp.where(lane == HALF, column, tail)
-    all_ref[mine, COLUMNS - LANE : COLUMNS] = tail.astype(jnp.bfloat16)
-    here.add(("B1", 0, 0))
-    issue()
-    for chunk in CHUNKS:
-        hand_over((chunk, 0, 0))
-
+        for item in items:
+            hand_over(item)
+
+    def norm_copy(k):
+        return pltpu.make_async_remote_copy(
+            src_ref=nz.at[z], dst_ref=nz.at[z], send_sem=norm_send.at[k], recv_sem=norm_recv.at[z],
+            device_id={"zero": zero, "tp": k}, device_id_type=MESH,
+        )
+
+    pl.semaphore_wait(barrier, len(target) + 1 + z)
+    issue(("A0", 0, 0), ("B1", 0, 0))
+
+    up = latest(1, 2)
+    both = jnp.concatenate([gate[:, cut:], up], axis=1)
+    all_ref[mine, cut : 2 * WIDTH] = both.astype(jnp.bfloat16)
+    loads[9].wait()
+    loads[10].wait()
+    gain = (n[0] + n[1]).astype(jnp.bfloat16).astype(jnp.float32)
+    nz[z] = jnp.concatenate([gain, jnp.zeros((1, LANE - gain.shape[1]), jnp.float32)], axis=1)
+    issue(("A1", 0, 0), ("B0", 0, 0))
+
+    for k in range(tp - 1):
+
+        @pl.when(k < z)
+        def _():
+            pl.semaphore_signal(ready, inc=1, device_id={"zero": zero, "tp": k}, device_id_type=MESH)
+            norm_copy(k).start()
+
+    waited = 0
     for item in arrivals:
-        if item[1:] == (0, 0):
-            continue
-        part = span(item)
-        pltpu.make_async_remote_copy(
-            src_ref=part, dst_ref=part, send_sem=send_sem, recv_sem=recv_sem.at[number[item]],
-            device_id={"zero": peer, "tp": z}, device_id_type=MESH,
-        ).wait_recv()
-        here.add(item)
-        issue()
-        hand_over(item)
+        if item == ("C0", 0, 0):
+            for k in range(tp):
+
+                @pl.when(k != z)
+                def _():
+                    pltpu.make_async_remote_copy(
+                        src_ref=nz.at[k], dst_ref=nz.at[k], send_sem=norm_send.at[k], recv_sem=norm_recv.at[k],
+                        device_id={"zero": zero, "tp": k}, device_id_type=MESH,
+                    ).wait_recv()
+
+            row = lax.broadcasted_iota(jnp.int32, (BLOCK, LANE), 0)
+            lane = lax.broadcasted_iota(jnp.int32, (BLOCK, LANE), 1)
+            share = BLOCK // tp
+            picked = jnp.zeros((BLOCK, LANE), jnp.float32)
+            for k in range(tp):
+                own = (lane == row - k * share) & (lane < share)
+                picked = jnp.where(own, jnp.broadcast_to(nz[k], (BLOCK, LANE)), picked)
+            column = jnp.sum(picked, axis=1, keepdims=True)
+            tail = jnp.concatenate([down[:, cut:], jnp.zeros((BLOCK, HALF), jnp.float32)], axis=1)
+            tail = jnp.where(lane == HALF, column, tail)
+            all_ref[mine, COLUMNS - LANE : COLUMNS] = tail.astype(jnp.bfloat16)
+            issue(item)
+        elif item[1:] != (0, 0):
+            part = span(item)
+            pltpu.make_async_remote_copy(
+                src_ref=part, dst_ref=part, send_sem=send_sem, recv_sem=recv_sem.at[number[item]],
+                device_id={"zero": peer, "tp": z}, device_id_type=MESH,
+            ).wait_recv()
+            issue(item)
+            waited += 1
+            if waited == 8:
+
+                @pl.when(z < tp - 1)
+                def _():
+                    pl.semaphore_wait(ready, tp - 1 - z)
+
+                for k in range(1, tp):
+
+                    @pl.when(k > z)
+                    def _():
+                        norm_copy(k).start()
+
     assert not any(queue.values())
 
     blocks = SIDE * SIDE
     for sem, rows in ((peer_recv, blocks), (peer_send, blocks), (send_sem, blocks - 1)):
         whole = all_ref.at[0 : rows * BLOCK]
         pltpu.make_async_copy(whole, whole, sem).wait()
-    for copy in norm_copies:
-        copy.wait_send()
+    for k in range(tp):
+
+        @pl.when(k != z)
+        def _():
+            norm_copy(k).wait_send()
 
 
 def turn_kernel(all_ref, gate, up, down, norm, stage, norm_rows, sem, norm_sem):
@@ -282,8 +313,9 @@
             pltpu.VMEM((8, 1, LANE), jnp.float32),
             pltpu.SemaphoreType.DMA((11,)),
             pltpu.SemaphoreType.DMA((items,)),
-            pltpu.SemaphoreType.DMA((7,)),
-            pltpu.SemaphoreType.DMA((7,)),
+            pltpu.SemaphoreType.DMA((8,)),
+            pltpu.SemaphoreType.DMA((8,)),
+            pltpu.SemaphoreType.REGULAR,
             pltpu.SemaphoreType.DMA,
             pltpu.SemaphoreType.DMA,
             pltpu.SemaphoreType.DMA,

time: 70.5 us -> 65.3 us (0.926)
  Pallas kernels: 69.7 us -> 64.6 us
    pallas_call x1, Pallas kernels: 62.8 us -> 57.7 us  [local(): pl.pallas_call(gather_kernel, out_shape=pltpu.VMEM((rows, COLUMNS), bf16)...]
where the time goes in v2:
time: 65.3 us; the launch traced here: 65.2 us
  Pallas kernels  64.6 us (99%)
    pallas_call x1, Pallas kernels, local(): pl.pallas_call(gather_kernel, out_shape=pltpu.VMEM((rows, COLUMNS), bf16)...  57.7 us
    pallas_call x1, Pallas kernels, local(): pl.pallas_call(turn_kernel, out_shape=[jax.ShapeDtypeStruct((WIDTH, rows)...  6.93 us

profile of v2, /device:TPU:1, one launch (start us, length us, event | category | flops | bytes accessed | tf_op | source)
XLA Modules:
  0.0 65.2 jit_solution(11586462501232728606)
XLA Ops:
  0.6 57.7 %gather.1.all_ref = bf16[2560,3712]{1,0:T(8,128)(2,1)S(1)} custom-call(bf16[80,1216]{1,0:T(8,128)(2,1)} %wg.1, bf16[16,80]{1,0:T(8,128)(2,1)} %bitcast.11, bf16[16,1216]{1,0:T(8,128)(2,1)} %bg.1, bf16[80,1216]{1,0:T(8,128)(2,1)} %wu.1, bf16[16,80]{1,0:T(8,128)(2,1)} %bitcast.12, bf16[16,1216]{1,0:T(8,128)(2,1)} %bu.1, bf16[80,1216]{1,0:T(8,128)(2,1)} %bitcast.9, ...), custom_call_target="tpu_custom_call" | custom-call | tf_op jit(solution)/shard_map/gather/pallas_call | solution.py:303
  58.3 6.9 %turn.1 = (bf16[1216,2560]{1,0:T(8,128)(2,1)}, bf16[1216,2560]{1,0:T(8,128)(2,1)}, bf16[1216,2560]{1,0:T(8,128)(2,1)}, bf16[20,128]{1,0:T(8,128)(2,1)}) custom-call(bf16[2560,3712]{1,0:T(8,128)(2,1)S(1)} %gather.1.all_ref), custom_call_target="tpu_custom_call" | custom-call | tf_op jit(solution)/shard_map/turn/pallas_call | solution.py:326

commit v3 on v2

--- a/solution.py
+++ b/solution.py
@@ -15,12 +15,11 @@
 WIDTH = 1216
 RANK = 16
 LANE = 128
-CHUNKS = {"A0": (0, 7), "B1": (21, 28), "A1": (7, 14), "B0": (14, 21), "C0": (28, 29)}
-OWN_US = {"A0": 0.0, "B1": 0.0, "A1": 0.6, "B0": 0.6, "C0": 20.0}
-TILES = 29
-COLUMNS = TILES * LANE
-NORM_LANE = 3 * WIDTH
+CHUNKS = {"A0": (0, 7), "B1": (21, 28), "A1": (7, 14), "B0": (14, 21), "C0": None}
+OWN_US = {"A0": 0.0, "B1": 0.0, "A1": 0.6, "B0": 0.6, "C0": 15.0}
+COLUMNS = 28 * LANE
 HALF = LANE // 2
+FOLD = 48
 
 mix_rate = 0.5
 
@@ -60,14 +59,15 @@
         if item is not None:
             arrivals.append(item)
             for link in onward(item):
-                heapq.heappush(ready[link], (-depth(seen_there(item, link)), count, item))
+                urgent = depth(seen_there(item, link)) if CHUNKS[item[0]] else 9
+                heapq.heappush(ready[link], (-urgent, count, item))
                 count += 1
         if events and events[0][0] <= now + 1e-9:
             continue
         for link in LINKS:
             if free[link] <= now + 1e-9 and ready[link]:
                 item = heapq.heappop(ready[link])[2]
-                lo, hi = CHUNKS[item[0]]
+                lo, hi = CHUNKS[item[0]] or (0, 0.6)
                 free[link] = now + (hi - lo) * tile_us
                 sends[link].append(item)
                 heapq.heappush(events, (free[link], count, None))
@@ -77,8 +77,9 @@
 
 
 def gather_kernel(
-    wg, ag, bg, wu, au, bu, wd, ad, bd, nt, ns, all_ref,
-    w, a, b, n, nz, in_sem, recv_sem, norm_send, norm_recv, ready, send_sem, peer_send, peer_recv,
+    wg, ag, bg, wu, au, bu, wd, ad, bd, nt, ns, all_ref, rest, norm,
+    w, a, b, n, nz, folded, picks, flat,
+    in_sem, recv_sem, norm_send, norm_recv, ready, send_sem, peer_send, peer_recv,
 ):
     zero, z = lax.axis_index("zero"), lax.axis_index("tp")
     tp = lax.axis_size("tp")
@@ -135,8 +136,13 @@
     sends, arrivals = plan()
     number = {item: k for k, item in enumerate(i for i in arrivals if i[1:] != (0, 0))}
 
+    def kind(item):
+        return int(CHUNKS[item[0]] is None)
+
     def span(item):
         chunk, ou, ov = item
+        if CHUNKS[chunk] is None:
+            return folded.at[pl.ds(pl.multiple_of(place[ou, ov] * FOLD, 16), FOLD)]
         lo, hi = CHUNKS[chunk]
         rows = pl.ds(pl.multiple_of(place[ou, ov] * BLOCK, 16), BLOCK)
         return all_ref.at[rows, lo * LANE : hi * LANE]
@@ -144,14 +150,14 @@
     def send(item, link):
         part = span(item)
         pltpu.make_async_remote_copy(
-            src_ref=part, dst_ref=part, send_sem=send_sem, recv_sem=recv_sem.at[number[seen_there(item, link)]],
+            src_ref=part, dst_ref=part, send_sem=send_sem.at[kind(item)], recv_sem=recv_sem.at[number[seen_there(item, link)]],
             device_id={"zero": target[link], "tp": z}, device_id_type=MESH,
         ).start()
 
     def hand_over(item):
         part = span(item)
         pltpu.make_async_remote_copy(
-            src_ref=part, dst_ref=part, send_sem=peer_send, recv_sem=peer_recv,
+            src_ref=part, dst_ref=part, send_sem=peer_send.at[kind(item)], recv_sem=peer_recv.at[kind(item)],
             device_id={"zero": peer, "tp": z}, device_id_type=MESH,
         ).start()
 
@@ -195,7 +201,36 @@
             pl.semaphore_signal(ready, inc=1, device_id={"zero": zero, "tp": k}, device_id_type=MESH)
             norm_copy(k).start()
 
-    waited = 0
+    wide = 8 * BLOCK
+
+    def make_picks():
+        for e in range(8):
+            r = lax.broadcasted_iota(jnp.int32, (FOLD, wide), 0)
+            c = lax.broadcasted_iota(jnp.int32, (FOLD, wide), 1) - e * BLOCK
+            half = BLOCK // 2
+            for m, hit in enumerate(
+                [(c == r) & (r < half), (c == r + half) & (r < half), (r == half) & (c >= 0) & (c < BLOCK)]
+            ):
+                picks[m, e * FOLD : (e + 1) * FOLD] = jnp.where(hit, 1.0, 0.0).astype(jnp.bfloat16)
+
+    def unfold(g):
+        rows = folded[g * 8 * FOLD : (g + 1) * 8 * FOLD]
+        left, right, line = (
+            lax.dot_general(rows, picks[m], (((0,), (0,)), ((), ())), preferred_element_type=jnp.float32)
+            for m in range(3)
+        )
+        rest[:, g * wide : (g + 1) * wide] = (left[:HALF] + right[HALF:]).astype(jnp.bfloat16)
+        i = lax.broadcasted_iota(jnp.int32, (BLOCK, wide), 0)
+        l = lax.broadcasted_iota(jnp.int32, (BLOCK, wide), 1)
+        own = functools.reduce(jnp.logical_or, [i + e * BLOCK == l for e in range(8)])
+        gains = jnp.sum(jnp.where(own, line[:BLOCK], 0.0), axis=0, keepdims=True)
+        for k in range(wide // LANE):
+            at_row = g * (wide // LANE) + k
+            flat[at_row : at_row + 1] = gains[:, k * LANE : (k + 1) * LANE]
+
+    c_left = sum(kind(item) for item in arrivals) - 1
+    groups = list(range(all_ref.shape[0] // wide))
+    waited, stored = 0, []
     for item in arrivals:
         if item == ("C0", 0, 0):
             for k in range(tp):
@@ -207,26 +242,33 @@
                         device_id={"zero": zero, "tp": k}, device_id_type=MESH,
                     ).wait_recv()
 
-            row = lax.broadcasted_iota(jnp.int32, (BLOCK, LANE), 0)
-            lane = lax.broadcasted_iota(jnp.int32, (BLOCK, LANE), 1)
             share = BLOCK // tp
-            picked = jnp.zeros((BLOCK, LANE), jnp.float32)
-            for k in range(tp):
-                own = (lane == row - k * share) & (lane < share)
-                picked = jnp.where(own, jnp.broadcast_to(nz[k], (BLOCK, LANE)), picked)
-            column = jnp.sum(picked, axis=1, keepdims=True)
-            tail = jnp.concatenate([down[:, cut:], jnp.zeros((BLOCK, HALF), jnp.float32)], axis=1)
-            tail = jnp.where(lane == HALF, column, tail)
-            all_ref[mine, COLUMNS - LANE : COLUMNS] = tail.astype(jnp.bfloat16)
-            issue(item)
+            gains = [nz[k][:, :share] for k in range(tp)] + [jnp.zeros((1, LANE - BLOCK), jnp.float32)]
+            gains = jnp.concatenate(gains, axis=1)
+            left = down[:, cut:]
+            top = jnp.concatenate([left[: BLOCK // 2], left[BLOCK // 2 :]], axis=1)
+            line = lax.broadcasted_iota(jnp.int32, (FOLD - BLOCK // 2, LANE), 0)
+            bottom = jnp.where(line == 0, jnp.broadcast_to(gains, line.shape), 0.0)
+            fold = jnp.concatenate([top, bottom], axis=0).astype(jnp.bfloat16)
+            folded[pl.ds(pl.multiple_of(zero * FOLD, 16), FOLD)] = fold
+            stored.append(item)
         elif item[1:] != (0, 0):
             part = span(item)
             pltpu.make_async_remote_copy(
-                src_ref=part, dst_ref=part, send_sem=send_sem, recv_sem=recv_sem.at[number[item]],
+                src_ref=part, dst_ref=part, send_sem=send_sem.at[kind(item)], recv_sem=recv_sem.at[number[item]],
                 device_id={"zero": peer, "tp": z}, device_id_type=MESH,
             ).wait_recv()
-            issue(item)
+            issue(item, *stored)
+            stored.clear()
             waited += 1
+            c_left -= kind(item)
+            if waited == 6:
+                make_picks()
+            if c_left == 0 and kind(item):
+                folds = folded.at[0 : SIDE * SIDE * FOLD]
+                pltpu.make_async_copy(folds, folds, peer_recv.at[1]).wait()
+            elif c_left == 0 and groups:
+                unfold(groups.pop(0))
             if waited == 8:
 
                 @pl.when(z < tp - 1)
@@ -239,11 +281,18 @@
                     def _():
                         norm_copy(k).start()
 
-    assert not any(queue.values())
-
+    assert not any(queue.values()) and not groups
+
+    norm[...] = flat[0 : norm.shape[0]].astype(jnp.bfloat16)
     blocks = SIDE * SIDE
-    for sem, rows in ((peer_recv, blocks), (peer_send, blocks), (send_sem, blocks - 1)):
-        whole = all_ref.at[0 : rows * BLOCK]
+    for sem, count, buffer, rows in (
+        (peer_recv.at[0], blocks, all_ref, BLOCK),
+        (peer_send.at[0], blocks, all_ref, BLOCK),
+        (peer_send.at[1], blocks, folded, FOLD),
+        (send_sem.at[0], blocks - 1, all_ref, BLOCK),
+        (send_sem.at[1], blocks - 1, folded, FOLD),
+    ):
+        whole = buffer.at[0 : count * rows]
         pltpu.make_async_copy(whole, whole, sem).wait()
     for k in range(tp):
 
@@ -252,27 +301,31 @@
             norm_copy(k).wait_send()
 
 
-def turn_kernel(all_ref, gate, up, down, norm, stage, norm_rows, sem, norm_sem):
+def turn_kernel(all_ref, rest, norm_rows, gate, up, down, norm, stage, sem, rest_sem):
     outs = (gate, up, down)
     total = all_ref.shape[0]
     size, step = stage.shape[1], LANE
-    starts = list(range(0, COLUMNS, size))
+    lasts = [
+        pltpu.make_async_copy(rest, down.at[WIDTH - HALF : WIDTH], rest_sem.at[0]),
+        pltpu.make_async_copy(norm_rows, norm, rest_sem.at[1]),
+    ]
+    for copy in lasts:
+        copy.start()
     pending = {}
-    for order, start in enumerate(starts[-1:] + starts[:-1]):
-        wide = min(size, COLUMNS - start)
+    for order, start in enumerate(range(0, COLUMNS, size)):
         slot = order % stage.shape[0]
         for copy in pending.pop(slot, ()):
             copy.wait()
 
         def body(i, carry):
             rows = pl.ds(pl.multiple_of(i * step, step), step)
-            stage[slot, 0:wide, rows] = all_ref[rows, start : start + wide].T
+            stage[slot, :, rows] = all_ref[rows, start : start + size].T
             return carry
 
         lax.fori_loop(0, total // step, body, 0, unroll=True)
         started = []
         for t in range(3):
-            lo, hi = max(start, t * WIDTH), min(start + wide, (t + 1) * WIDTH)
+            lo, hi = max(start, t * WIDTH), min(start + size, (t + 1) * WIDTH)
             if lo < hi:
                 copy = pltpu.make_async_copy(
                     stage.at[slot, lo - start : hi - start],
@@ -281,15 +334,8 @@
                 )
                 copy.start()
                 started.append(copy)
-        if start <= NORM_LANE < start + wide:
-            row = stage[slot, NORM_LANE - start : NORM_LANE - start + 1, :].astype(jnp.float32)
-            pieces = [row[:, k : k + LANE] for k in range(0, total, LANE)]
-            norm_rows[...] = jnp.concatenate(pieces, axis=0).astype(jnp.bfloat16)
-            copy = pltpu.make_async_copy(norm_rows, norm, norm_sem)
-            copy.start()
-            started.append(copy)
         pending[slot] = started
-    for started in pending.values():
+    for started in [lasts, *pending.values()]:
         for copy in started:
             copy.wait()
 
@@ -300,43 +346,51 @@
     hbm = pl.BlockSpec(memory_space=pltpu.HBM)
     inputs = (wg, ag.T, bg, wu, au.T, bu, wd.T, bd, ad.T, nt.reshape(1, -1), ns.reshape(1, -1))
     items = len(CHUNKS) * (SIDE * SIDE - 1)
+    vmem = pl.BlockSpec(memory_space=pltpu.VMEM)
+    flat_rows = rows // LANE
     gathered = pl.pallas_call(
         gather_kernel,
-        out_shape=pltpu.VMEM((rows, COLUMNS), bf16),
+        out_shape=[
+            pltpu.VMEM((rows, COLUMNS), bf16),
+            pltpu.VMEM((HALF, rows), bf16),
+            pltpu.VMEM((flat_rows, LANE), bf16),
+        ],
         in_specs=[hbm] * 11,
-        out_specs=pl.BlockSpec(memory_space=pltpu.VMEM),
+        out_specs=[vmem] * 3,
         scratch_shapes=[
             pltpu.VMEM((3, BLOCK, WIDTH), bf16),
             pltpu.VMEM((3, RANK, BLOCK), bf16),
             pltpu.VMEM((3, RANK, WIDTH), bf16),
             pltpu.VMEM((2, 1, nt.shape[0]), jnp.float32),
             pltpu.VMEM((8, 1, LANE), jnp.float32),
+            pltpu.VMEM((2 * SIDE * SIDE * FOLD, LANE), bf16),
+            pltpu.VMEM((3, 8 * FOLD, 8 * BLOCK), bf16),
+            pltpu.VMEM((24, LANE), jnp.float32),
             pltpu.SemaphoreType.DMA((11,)),
             pltpu.SemaphoreType.DMA((items,)),
             pltpu.SemaphoreType.DMA((8,)),
             pltpu.SemaphoreType.DMA((8,)),
             pltpu.SemaphoreType.REGULAR,
-            pltpu.SemaphoreType.DMA,
-            pltpu.SemaphoreType.DMA,
-            pltpu.SemaphoreType.DMA,
+            pltpu.SemaphoreType.DMA((2,)),
+            pltpu.SemaphoreType.DMA((2,)),
+            pltpu.SemaphoreType.DMA((2,)),
         ],
         compiler_params=pltpu.CompilerParams(collective_id=0, has_side_effects=True, vmem_limit_bytes=16 << 20),
         name="gather",
     )(*(pltpu.with_memory_space_constraint(v, pltpu.HBM) for v in inputs))
     gate, up, down, norm = pl.pallas_call(
         turn_kernel,
-        out_shape=[jax.ShapeDtypeStruct((WIDTH, rows), bf16)] * 3 + [jax.ShapeDtypeStruct((rows // LANE, LANE), bf16)],
-        in_specs=[pl.BlockSpec(memory_space=pltpu.VMEM)],
+        out_shape=[jax.ShapeDtypeStruct((WIDTH, rows), bf16)] * 3 + [jax.ShapeDtypeStruct((flat_rows, LANE), bf16)],
+        in_specs=[vmem] * 3,
         out_specs=[hbm] * 4,
         scratch_shapes=[
             pltpu.VMEM((4, 256, rows), bf16),
-            pltpu.VMEM((rows // LANE, LANE), bf16),
             pltpu.SemaphoreType.DMA((4, 2)),
-            pltpu.SemaphoreType.DMA,
+            pltpu.SemaphoreType.DMA((2,)),
         ],
         compiler_params=pltpu.CompilerParams(vmem_limit_bytes=16 << 20),
         name="turn",
-    )(gathered)
+    )(*gathered)
     return gate.T, up.T, down, norm.reshape(rows)
 
 

time: 65.3 us -> 65.5 us (level)
  no operation moved by 1% of the time
where the time goes in v3:
time: 65.5 us; the launch traced here: 65.4 us
  Pallas kernels  64.7 us (99%)
    pallas_call x1, Pallas kernels, local(): pl.pallas_call(gather_kernel, out_shape=[pltpu.VMEM((rows, COLUMNS), bf16...  57.9 us
    pallas_call x1, Pallas kernels, local(): pl.pallas_call(turn_kernel, out_shape=[jax.ShapeDtypeStruct((WIDTH, rows)...  6.77 us

profile of v3, /device:TPU:1, one launch (start us, length us, event | category | flops | bytes accessed | tf_op | source)
XLA Modules:
  0.0 65.4 jit_solution(3640614705349061794)
XLA Ops:
  0.6 57.9 %gather.1 = (bf16[2560,3584]{1,0:T(8,128)(2,1)S(1)}, bf16[64,2560]{1,0:T(8,128)(2,1)S(1)}, bf16[20,128]{1,0:T(8,128)(2,1)S(1)}) custom-call(bf16[80,1216]{1,0:T(8,128)(2,1)} %wg.1, bf16[16,80]{1,0:T(8,128)(2,1)} %bitcast.11, bf16[16,1216]{1,0:T(8,128)(2,1)} %bg.1, bf16[80,1216]{1,0:T(8,128)(2,1)} %wu.1, bf16[16,80]{1,0:T(8,128)(2,1)} %bitcast.12, ...), custom_call_target="tpu_custom_call" | custom-call | tf_op jit(solution)/shard_map/gather/pallas_call | solution.py:351
  58.6 6.8 %turn.1 = (bf16[1216,2560]{1,0:T(8,128)(2,1)}, bf16[1216,2560]{1,0:T(8,128)(2,1)}, bf16[1216,2560]{1,0:T(8,128)(2,1)}, bf16[20,128]{1,0:T(8,128)(2,1)}) custom-call(bf16[2560,3584]{1,0:T(8,128)(2,1)S(1)} %get-tuple-element.11.all_ref, bf16[64,2560]{1,0:T(8,128)(2,1)S(1)} %get-tuple-element.12.rest, bf16[20,128]{1,0:T(8,128)(2,1)S(1)} %get-tuple-element.13.norm_rows), custom_call_target="tpu_custom_call" | custom-call | tf_op jit(solution)/shard_map/turn/pallas_call | solution.py:381

commit v4 on v3

--- a/solution.py
+++ b/solution.py
@@ -46,7 +46,7 @@
     return max((1 + depth(seen_there(item, link)) for link in onward(item)), default=0)
 
 
-def plan(tile_us=0.44, hop_us=2.5):
+def plan(tile_us=0.44, hop_us=4.0):
     free = dict.fromkeys(LINKS, 0.0)
     ready = {link: [] for link in LINKS}
     sends = {link: [] for link in LINKS}
@@ -95,6 +95,15 @@
     target = {"u+": place[1, 0], "u-": place[3, 0], "v+": place[0, 1], "v-": place[0, 3]}
     peer = zero + 1 - 2 * core
 
+    barrier = pltpu.get_barrier_semaphore()
+    for other in list(target.values()) + [peer]:
+        pl.semaphore_signal(barrier, inc=1, device_id={"zero": other, "tp": z}, device_id_type=MESH)
+    for k in range(1, tp):
+
+        @pl.when(k > z)
+        def _():
+            pl.semaphore_signal(barrier, inc=1, device_id={"zero": zero, "tp": k}, device_id_type=MESH)
+
     loads = []
     for k, (src, dst) in enumerate(
         [
@@ -108,30 +117,28 @@
         load.start()
         loads.append(load)
 
-    barrier = pltpu.get_barrier_semaphore()
-    for other in list(target.values()) + [peer]:
-        pl.semaphore_signal(barrier, inc=1, device_id={"zero": other, "tp": z}, device_id_type=MESH)
-    for k in range(1, tp):
-
-        @pl.when(k > z)
-        def _():
-            pl.semaphore_signal(barrier, inc=1, device_id={"zero": zero, "tp": k}, device_id_type=MESH)
-
     mine = pl.ds(pl.multiple_of(zero * BLOCK, 16), BLOCK)
     cut = WIDTH - HALF
 
-    def latest(t, order):
+    def latest(t, lo, hi):
+        low_high = lax.dot_general(
+            a[t], b[t, :, lo:hi], (((0,), (0,)), ((), ())), preferred_element_type=jnp.float32
+        )
+        return w[t, :, lo:hi].astype(jnp.float32) + mix_rate * low_high
+
+    def keep(first, value):
+        all_ref[mine, first : first + value.shape[1]] = value.astype(jnp.bfloat16)
+
+    def arrive(order):
         for load in loads[3 * order : 3 * order + 3]:
             load.wait()
-        low_high = lax.dot_general(
-            a[t], b[t], (((0,), (0,)), ((), ())), preferred_element_type=jnp.float32
-        )
-        return w[t].astype(jnp.float32) + mix_rate * low_high
-
-    gate = latest(0, 0)
-    all_ref[mine, 0:cut] = gate[:, :cut].astype(jnp.bfloat16)
-    down = latest(2, 1)
-    all_ref[mine, 2 * WIDTH : 2 * WIDTH + cut] = down[:, :cut].astype(jnp.bfloat16)
+
+    head = CHUNKS["A0"][1] * LANE
+    back = CHUNKS["B1"][0] * LANE - 2 * WIDTH
+    arrive(0)
+    keep(0, latest(0, 0, head))
+    arrive(1)
+    keep(2 * WIDTH + back, latest(2, back, cut))
 
     sends, arrivals = plan()
     number = {item: k for k, item in enumerate(i for i in arrivals if i[1:] != (0, 0))}
@@ -185,9 +192,9 @@
     pl.semaphore_wait(barrier, len(target) + 1 + z)
     issue(("A0", 0, 0), ("B1", 0, 0))
 
-    up = latest(1, 2)
-    both = jnp.concatenate([gate[:, cut:], up], axis=1)
-    all_ref[mine, cut : 2 * WIDTH] = both.astype(jnp.bfloat16)
+    keep(2 * WIDTH, latest(2, 0, back))
+    arrive(2)
+    keep(head, jnp.concatenate([latest(0, head, WIDTH), latest(1, 0, WIDTH)], axis=1))
     loads[9].wait()
     loads[10].wait()
     gain = (n[0] + n[1]).astype(jnp.bfloat16).astype(jnp.float32)
@@ -245,7 +252,7 @@
             share = BLOCK // tp
             gains = [nz[k][:, :share] for k in range(tp)] + [jnp.zeros((1, LANE - BLOCK), jnp.float32)]
             gains = jnp.concatenate(gains, axis=1)
-            left = down[:, cut:]
+            left = latest(2, cut, WIDTH)
             top = jnp.concatenate([left[: BLOCK // 2], left[BLOCK // 2 :]], axis=1)
             line = lax.broadcasted_iota(jnp.int32, (FOLD - BLOCK // 2, LANE), 0)
             bottom = jnp.where(line == 0, jnp.broadcast_to(gains, line.shape), 0.0)
@@ -312,20 +319,22 @@
     for copy in lasts:
         copy.start()
     pending = {}
-    for order, start in enumerate(range(0, COLUMNS, size)):
+    half = size // 2
+    blocks = [(0, half), (half, half)] + [(start, size) for start in range(size, COLUMNS, size)]
+    for order, (start, wide) in enumerate(blocks):
         slot = order % stage.shape[0]
         for copy in pending.pop(slot, ()):
             copy.wait()
 
         def body(i, carry):
             rows = pl.ds(pl.multiple_of(i * step, step), step)
-            stage[slot, :, rows] = all_ref[rows, start : start + size].T
+            stage[slot, 0:wide, rows] = all_ref[rows, start : start + wide].T
             return carry
 
         lax.fori_loop(0, total // step, body, 0, unroll=True)
         started = []
         for t in range(3):
-            lo, hi = max(start, t * WIDTH), min(start + size, (t + 1) * WIDTH)
+            lo, hi = max(start, t * WIDTH), min(start + wide, (t + 1) * WIDTH)
             if lo < hi:
                 copy = pltpu.make_async_copy(
                     stage.at[slot, lo - start : hi - start],

time: 65.5 us -> 64.5 us (0.985)
  Pallas kernels: 64.7 us -> 63.7 us
    pallas_call x1, Pallas kernels: 57.9 us -> 57.1 us  [local(): pl.pallas_call(gather_kernel, out_shape=[pltpu.VMEM((rows, COLUMNS), bf16...]
where the time goes in v4:
time: 64.5 us; the launch traced here: 64.4 us
  Pallas kernels  63.7 us (99%)
    pallas_call x1, Pallas kernels, local(): pl.pallas_call(gather_kernel, out_shape=[pltpu.VMEM((rows, COLUMNS), bf16...  57.1 us
    pallas_call x1, Pallas kernels, local(): pl.pallas_call(turn_kernel, out_shape=[jax.ShapeDtypeStruct((WIDTH, rows)...  6.68 us

profile of v4, /device:TPU:1, one launch (start us, length us, event | category | flops | bytes accessed | tf_op | source)
XLA Modules:
  0.0 64.4 jit_solution(12782466106999151830)
XLA Ops:
  0.6 57.1 %gather.1 = (bf16[2560,3584]{1,0:T(8,128)(2,1)S(1)}, bf16[64,2560]{1,0:T(8,128)(2,1)S(1)}, bf16[20,128]{1,0:T(8,128)(2,1)S(1)}) custom-call(bf16[80,1216]{1,0:T(8,128)(2,1)} %wg.1, bf16[16,80]{1,0:T(8,128)(2,1)} %bitcast.11, bf16[16,1216]{1,0:T(8,128)(2,1)} %bg.1, bf16[80,1216]{1,0:T(8,128)(2,1)} %wu.1, bf16[16,80]{1,0:T(8,128)(2,1)} %bitcast.12, ...), custom_call_target="tpu_custom_call" | custom-call | tf_op jit(solution)/shard_map/gather/pallas_call | solution.py:360
  57.7 6.7 %turn.1 = (bf16[1216,2560]{1,0:T(8,128)(2,1)}, bf16[1216,2560]{1,0:T(8,128)(2,1)}, bf16[1216,2560]{1,0:T(8,128)(2,1)}, bf16[20,128]{1,0:T(8,128)(2,1)}) custom-call(bf16[2560,3584]{1,0:T(8,128)(2,1)S(1)} %get-tuple-element.11.all_ref, bf16[64,2560]{1,0:T(8,128)(2,1)S(1)} %get-tuple-element.12.rest, bf16[20,128]{1,0:T(8,128)(2,1)S(1)} %get-tuple-element.13.norm_rows), custom_call_target="tpu_custom_call" | custom-call | tf_op jit(solution)/shard_map/turn/pallas_call | solution.py:390

commit v5 on v4

--- a/solution.py
+++ b/solution.py
@@ -46,7 +46,7 @@
     return max((1 + depth(seen_there(item, link)) for link in onward(item)), default=0)
 
 
-def plan(tile_us=0.44, hop_us=4.0):
+def plan(tile_us=0.44, hop_us=4.0, leaf_us=3.0):
     free = dict.fromkeys(LINKS, 0.0)
     ready = {link: [] for link in LINKS}
     sends = {link: [] for link in LINKS}
@@ -57,7 +57,8 @@
     while events:
         now, _, item = heapq.heappop(events)
         if item is not None:
-            arrivals.append(item)
+            arrivals.append((now + (0.0 if onward(item) else leaf_us), count, item))
+            count += 1
             for link in onward(item):
                 urgent = depth(seen_there(item, link)) if CHUNKS[item[0]] else 9
                 heapq.heappush(ready[link], (-urgent, count, item))
@@ -73,7 +74,7 @@
                 heapq.heappush(events, (free[link], count, None))
                 heapq.heappush(events, (free[link] + hop_us, count + 1, seen_there(item, link)))
                 count += 2
-    return sends, arrivals
+    return sends, [item for _, _, item in sorted(arrivals)]
 
 
 def gather_kernel(

time: 64.5 us -> 64.5 us (level)
  no operation moved by 1% of the time
where the time goes in v5:
time: 64.5 us; the launch traced here: 64.4 us
  Pallas kernels  63.7 us (99%)
    pallas_call x1, Pallas kernels, local(): pl.pallas_call(gather_kernel, out_shape=[pltpu.VMEM((rows, COLUMNS), bf16...  57.1 us
    pallas_call x1, Pallas kernels, local(): pl.pallas_call(turn_kernel, out_shape=[jax.ShapeDtypeStruct((WIDTH, rows)...  6.68 us

profile of v5, /device:TPU:1, one launch (start us, length us, event | category | flops | bytes accessed | tf_op | source)
XLA Modules:
  0.0 64.4 jit_solution(10340333208039776944)
XLA Ops:
  0.6 57.1 %gather.1 = (bf16[2560,3584]{1,0:T(8,128)(2,1)S(1)}, bf16[64,2560]{1,0:T(8,128)(2,1)S(1)}, bf16[20,128]{1,0:T(8,128)(2,1)S(1)}) custom-call(bf16[80,1216]{1,0:T(8,128)(2,1)} %wg.1, bf16[16,80]{1,0:T(8,128)(2,1)} %bitcast.11, bf16[16,1216]{1,0:T(8,128)(2,1)} %bg.1, bf16[80,1216]{1,0:T(8,128)(2,1)} %wu.1, bf16[16,80]{1,0:T(8,128)(2,1)} %bitcast.12, ...), custom_call_target="tpu_custom_call" | custom-call | tf_op jit(solution)/shard_map/gather/pallas_call | solution.py:361
  57.7 6.7 %turn.1 = (bf16[1216,2560]{1,0:T(8,128)(2,1)}, bf16[1216,2560]{1,0:T(8,128)(2,1)}, bf16[1216,2560]{1,0:T(8,128)(2,1)}, bf16[20,128]{1,0:T(8,128)(2,1)}) custom-call(bf16[2560,3584]{1,0:T(8,128)(2,1)S(1)} %get-tuple-element.11.all_ref, bf16[64,2560]{1,0:T(8,128)(2,1)S(1)} %get-tuple-element.12.rest, bf16[20,128]{1,0:T(8,128)(2,1)S(1)} %get-tuple-element.13.norm_rows), custom_call_target="tpu_custom_call" | custom-call | tf_op jit(solution)/shard_map/turn/pallas_call | solution.py:391
